TPU v7x, 32 devices: a whole 2x2x4 slice. The times are simulated.
32 devices in a mesh: gx: 4 (over x, core), gy: 8 (over z, y).
Axes of the slice: x: 2, y: 2, z: 4, core: 2. Of those that a mesh axis runs over, the one named last changes fastest.
Arguments:
- right_side: float32 [2, 64, 256, 128], P(None, 'gx', 'gy'), may hold values from -6 to 6
- wavenumber: float32 [64, 256, 128], P('gx', 'gy'), may hold values from 0.2 to 1
- pml_layer: int32 [64, 256, 128], P('gx', 'gy'), may hold values from 0 to 3
- aggregate: int32 [64, 256, 128], P('gx', 'gy'), may hold values from 0 to 15, as said below
- coarse_inverse: float32 [2, 512, 512], P(None, ('gx', 'gy')), may hold values from -0.0029296875 to 0.0029296875
Outputs:
- solution: float32 [2, 64, 256, 128], P(None, 'gx', 'gy')
- hessenberg: float32 [2, 5, 4], replicated
Inputs may be any that keep to these rules, and one draw needn't show every extreme that they name: `aggregate`: along the third dimension the value never falls, and every value of 0 to 15 occurs in every column of cells.
All inputs are finite; a program needn't handle non-finite values.
Results may differ from a plain program's by a relative error of at most 0.00015.
Values sent between devices are 32-bit elements; how exact they have to be, the bound alone decides.
No kernel may reach another device: no remote copies, remote signals or barrier semaphores. Data moves between devices by JAX's collectives and lax.ppermute only.
A program may use at most 64 MiB of HBM per device.

v0:
```python
import math
import jax
import jax.numpy as jnp
from jax import lax
from jax.sharding import PartitionSpec as P

ITERS = 4
damping = 0.8
pml_strength = 3.0
epsilon = 1e-06


def with_halo(block, sides, width):
    for axis, dim in sides:
        count = lax.axis_size(axis)
        forward = [(i, i + 1) for i in range(count - 1)]
        backward = [(target, source) for source, target in forward]
        low = lax.ppermute(
            lax.slice_in_dim(block, block.shape[dim] - width, None, axis=dim), axis, forward
        )
        high = lax.ppermute(lax.slice_in_dim(block, 0, width, axis=dim), axis, backward)
        block = jnp.concatenate([low, block, high], axis=dim)
    return block


def coefficients(wavenumber, layer_float):
    wave_sq = wavenumber * wavenumber
    depth = layer_float / 3.0
    absorb = wave_sq * (pml_strength * depth * depth)
    diag_re = 6.0 - wave_sq
    magnitude = diag_re * diag_re + absorb * absorb
    return (wave_sq, absorb, damping * diag_re / magnitude, damping * absorb / magnitude)


def operate_inner(extended, wave_sq, absorb):
    middle = extended[:, 1:-1, 1:-1]
    above = jnp.concatenate([middle[..., 1:], jnp.zeros_like(middle[..., :1])], -1)
    below = jnp.concatenate([jnp.zeros_like(middle[..., :1]), middle[..., :-1]], -1)
    beside = (
        extended[:, 2:, 1:-1]
        + extended[:, :-2, 1:-1]
        + extended[:, 1:-1, 2:]
        + extended[:, 1:-1, :-2]
        + above
        + below
    )
    real_part = (6.0 - wave_sq) * middle[0] - beside[0] + absorb * middle[1]
    imag_part = (6.0 - wave_sq) * middle[1] - beside[1] - absorb * middle[0]
    return jnp.stack([real_part, imag_part])


def smooth(field, scale_re, scale_im):
    return jnp.stack(
        [scale_re * field[0] - scale_im * field[1], scale_re * field[1] + scale_im * field[0]]
    )


def complex_scale(scale_re, scale_im, field):
    return jnp.stack(
        [scale_re * field[0] - scale_im * field[1], scale_re * field[1] + scale_im * field[0]]
    )


def inner_local(left, right):
    return jnp.stack(
        [
            jnp.sum(left[0] * right[0] + left[1] * right[1]),
            jnp.sum(left[0] * right[1] - left[1] * right[0]),
        ]
    )


def least_squares(hessenberg, beta):
    real_h = hessenberg[0]
    imag_h = hessenberg[1]
    stacked = jnp.concatenate(
        [jnp.concatenate([real_h, -imag_h], 1), jnp.concatenate([imag_h, real_h], 1)], 0
    )
    count = stacked.shape[1]
    target = jnp.zeros((stacked.shape[0],), jnp.float32).at[0].set(beta)
    ortho = []
    upper = {}
    for column in range(count):
        vector = stacked[:, column]
        for position in range(column):
            upper[position, column] = jnp.zeros((), jnp.float32)
        for repeat in range(2):
            for position in range(len(ortho)):
                weight = jnp.sum(ortho[position] * vector)
                vector = vector - weight * ortho[position]
                upper[position, column] = upper[position, column] + weight
        norm_value = jnp.sqrt(jnp.sum(vector * vector))
        upper[column, column] = norm_value
        ortho.append(vector / norm_value)
    project = [jnp.sum(basis_vec * target) for basis_vec in ortho]
    solved = [None] * count
    for column in reversed(range(count)):
        total = project[column]
        for later in range(column + 1, count):
            total = total - upper[column, later] * solved[later]
        solved[column] = total / upper[column, column]
    return solved


def restrict(flat_field, flat_ids, levels_count):
    total = flat_ids.shape[0]
    block = math.gcd(total, 16384)
    levels = jnp.arange(levels_count, dtype=jnp.int32)

    def accumulate(step_index, result):
        piece = lax.dynamic_slice_in_dim(flat_field, step_index * block, block, 1)
        labels = lax.dynamic_slice_in_dim(flat_ids, step_index * block, block, 0)
        onehot = (labels[None, :] == levels[:, None]).astype(jnp.float32)
        return result + lax.dot_general(
            piece, onehot, (((1,), (1,)), ((), ())), precision=lax.Precision.HIGHEST
        )

    return lax.fori_loop(0, total // block, accumulate, jnp.zeros((2, levels_count), jnp.float32))


def prolong(values, flat_ids):
    total = flat_ids.shape[0]
    block = math.gcd(total, 16384)
    levels = jnp.arange(values.shape[1], dtype=jnp.int32)

    def place(step_index, result):
        labels = lax.dynamic_slice_in_dim(flat_ids, step_index * block, block, 0)
        onehot = (levels[:, None] == labels[None, :]).astype(jnp.float32)
        piece = jnp.dot(values, onehot, precision=lax.Precision.HIGHEST)
        return lax.dynamic_update_slice_in_dim(result, piece, step_index * block, 1)

    return lax.fori_loop(0, total // block, place, jnp.zeros((2, total), jnp.float32))


def coarse_fix(remainder, flat_ids, coarse_inverse):
    highest = lax.Precision.HIGHEST
    levels_count = coarse_inverse.shape[1]
    total_coarse = coarse_inverse.shape[2]
    partial_value = restrict(remainder.reshape(2, -1), flat_ids, levels_count)
    offset = (lax.axis_index("gx") * lax.axis_size("gy") + lax.axis_index("gy")) * levels_count
    padded = lax.dynamic_update_slice(
        jnp.zeros((2, total_coarse), jnp.float32), partial_value, (jnp.zeros((), jnp.int32), offset)
    )
    whole = lax.psum(padded, ("gx", "gy"))
    own_re = jnp.dot(coarse_inverse[0], whole[0], precision=highest) - jnp.dot(
        coarse_inverse[1], whole[1], precision=highest
    )
    own_im = jnp.dot(coarse_inverse[0], whole[1], precision=highest) + jnp.dot(
        coarse_inverse[1], whole[0], precision=highest
    )
    return prolong(jnp.stack([own_re, own_im]), flat_ids).reshape(remainder.shape)


def operate_near(field, wave_sq, absorb):
    extended = with_halo(field, (("gx", 1), ("gy", 2)), 1)
    return operate_inner(extended, wave_sq, absorb)


def operate_final(field, wave_sq, absorb):
    extended = with_halo(field, (("gx", 1), ("gy", 2)), 1)
    return operate_inner(extended, wave_sq, absorb)


def body(right_side, wavenumber, pml_layer, aggregate, coarse_inverse):
    layer_float = pml_layer.astype(jnp.float32)
    wave_sq, absorb, scale_re, scale_im = coefficients(wavenumber, layer_float)
    flat_ids = aggregate.reshape(-1)
    beta = jnp.sqrt(lax.psum(jnp.sum(right_side * right_side), ("gx", "gy")) + epsilon)
    basis = [right_side / beta]
    directions = []
    columns_re = []
    columns_im = []
    for column in range(ITERS):
        vector = basis[column]
        first = smooth(vector, scale_re, scale_im)
        second = first + smooth(vector - operate_near(first, wave_sq, absorb), scale_re, scale_im)
        remainder = vector - operate_near(second, wave_sq, absorb)
        direction = second + coarse_fix(remainder, flat_ids, coarse_inverse)
        image = operate_final(direction, wave_sq, absorb)
        local_dots = jnp.stack([inner_local(member, image) for member in basis], 1)
        dots, squared = lax.psum((local_dots, jnp.sum(image * image)), ("gx", "gy"))
        for position in range(len(basis)):
            image = image - complex_scale(dots[0, position], dots[1, position], basis[position])
        leftover = squared - jnp.sum(dots * dots)
        length = jnp.sqrt(jnp.maximum(leftover, 0.0) + epsilon)
        tail = jnp.zeros((ITERS - 1 - column,), jnp.float32)
        columns_re.append(jnp.concatenate([dots[0], length[None], tail]))
        columns_im.append(jnp.concatenate([dots[1], jnp.zeros((1,), jnp.float32), tail]))
        directions.append(direction)
        if column + 1 < ITERS:
            basis.append(image / length)
    hessenberg = jnp.stack([jnp.stack(columns_re, 1), jnp.stack(columns_im, 1)])
    solved = least_squares(hessenberg, beta)
    solution = jnp.zeros_like(right_side)
    for column in range(ITERS):
        solution = solution + complex_scale(
            solved[column], solved[ITERS + column], directions[column]
        )
    return (solution, hessenberg)


def solution(mesh):
    return jax.shard_map(
        body,
        mesh=mesh,
        in_specs=(
            P(None, "gx", "gy", None),
            P("gx", "gy", None),
            P("gx", "gy", None),
            P("gx", "gy", None),
            P(None, ("gx", "gy"), None),
        ),
        out_specs=(P(None, "gx", "gy", None), P()),
        check_vma=False,
    )
```

profile of v0, /device:TPU:0, one launch (start us, length us, event | category | flops | bytes accessed | tf_op | source)
XLA Modules:
  0.0 809.6 jit_solution(285482413600228902)
XLA Ops:
  2.5 42.2 %psum.91 = f32[]{:T(128)} all-reduce(f32[]{:T(128)} %multiply_reduce_fusion.3), channel_id=1, replica_groups=mesh['gx'=4,'gy'=8] {'gx','gy'}, use_global_device_ids=true, to_apply=%region_1.0 | all-reduce | flops 1 | bytes 8 | tf_op jit(solution)/shard_map/psum | solution.py:168
  48.0 3.0 collective-permute-start.1
  53.2 5.0 collective-permute-start.3
  62.3 3.0 collective-permute-start.5
  67.5 5.4 collective-permute-start.7
  76.2 7.0 while.117
  83.3 46.5 %psum.92 = f32[2,512]{1,0:T(2,128)S(1)} all-reduce(f32[2,512]{1,0:T(2,128)S(1)} %dynamic_update_slice.40), channel_id=1, replica_groups=mesh['gx'=4,'gy'=8] {'gx','gy'}, use_global_device_ids=true, to_apply=%region_4.0 | all-reduce | flops 1024 | bytes 8192 | tf_op jit(solution)/shard_map/psum | solution.py:144
  134.9 3.0 collective-permute-start.9
  140.2 4.8 collective-permute-start.11
  149.7 43.8 %all-reduce.29 = (f32[2,1]{0,1:T(1,128)S(1)}, f32[]{:T(128)}) all-reduce(f32[2,1]{0,1:T(1,128)S(1)} %maximum_bitcast_fusion.1, f32[]{:T(128)} %multiply_reduce_fusion.2), channel_id=1, replica_groups=mesh['gx'=4,'gy'=8] {'gx','gy'}, use_global_device_ids=true, to_apply=%region_9.0 | all-reduce | flops 3 | bytes 24 | tf_op jit(solution)/shard_map/psum | solution.py:181
  199.2 3.0 collective-permute-start.13
  204.4 5.0 collective-permute-start.15
  214.4 3.4 collective-permute-start.17
  220.2 5.6 collective-permute-start.19
  228.3 2.1 divide_subtract_fusion.2
  230.3 6.9 while.118
  237.5 47.6 %psum.95 = f32[2,512]{1,0:T(2,128)S(1)} all-reduce(f32[2,512]{1,0:T(2,128)S(1)} %dynamic_update_slice.41), channel_id=1, replica_groups=mesh['gx'=4,'gy'=8] {'gx','gy'}, use_global_device_ids=true, to_apply=%region_15.0 | all-reduce | flops 1024 | bytes 8192 | tf_op jit(solution)/shard_map/psum | solution.py:144
  290.5 3.0 collective-permute-start.21
  295.7 4.8 collective-permute-start.23
  306.9 43.6 %all-reduce.28 = (f32[2,2]{0,1:T(2,128)S(1)}, f32[]{:T(128)}) all-reduce(f32[2,2]{0,1:T(2,128)S(1)} %pad_maximum_fusion.166, f32[]{:T(128)} %multiply_reduce_fusion.1), channel_id=1, replica_groups=mesh['gx'=4,'gy'=8] {'gx','gy'}, use_global_device_ids=true, to_apply=%region_22.0 | all-reduce | flops 5 | bytes 40 | tf_op jit(solution)/shard_map/psum | solution.py:181
  357.4 3.0 collective-permute-start.25
  362.6 5.0 collective-permute-start.27
  372.0 3.3 collective-permute-start.29
  377.5 5.3 collective-permute-start.31
  385.8 2.4 divide_subtract_fusion.1
  388.2 6.9 while.119
  395.3 47.6 %psum.98 = f32[2,512]{1,0:T(2,128)S(1)} all-reduce(f32[2,512]{1,0:T(2,128)S(1)} %dynamic_update_slice.42), channel_id=1, replica_groups=mesh['gx'=4,'gy'=8] {'gx','gy'}, use_global_device_ids=true, to_apply=%region_28.0 | all-reduce | flops 1024 | bytes 8192 | tf_op jit(solution)/shard_map/psum | solution.py:144
  448.4 3.0 collective-permute-start.33
  453.6 4.8 collective-permute-start.35
  467.3 43.7 %all-reduce.27 = (f32[2,3]{0,1:T(4,128)S(1)}, f32[]{:T(128)}) all-reduce(f32[2,3]{0,1:T(4,128)S(1)} %pad_maximum_fusion.161, f32[]{:T(128)} %multiply_reduce_fusion), channel_id=1, replica_groups=mesh['gx'=4,'gy'=8] {'gx','gy'}, use_global_device_ids=true, to_apply=%region_37.0 | all-reduce | flops 7 | bytes 56 | tf_op jit(solution)/shard_map/psum | solution.py:181
  513.7 2.5 multiply_subtract_fusion.5
  522.2 3.0 collective-permute-start.37
  528.0 5.1 collective-permute-start.39
  537.5 3.1 collective-permute-start.41
  542.8 5.5 collective-permute-start.43
  550.0 2.8 divide_subtract_fusion
  552.9 6.9 while.120
  560.0 47.0 %psum.101 = f32[2,512]{1,0:T(2,128)S(1)} all-reduce(f32[2,512]{1,0:T(2,128)S(1)} %dynamic_update_slice.43), channel_id=1, replica_groups=mesh['gx'=4,'gy'=8] {'gx','gy'}, use_global_device_ids=true, to_apply=%region_43.0 | all-reduce | flops 1024 | bytes 8192 | tf_op jit(solution)/shard_map/psum | solution.py:144
  608.5 4.3 while.116
  615.6 3.0 collective-permute-start.45
  620.8 4.8 collective-permute-start.47
  636.3 43.7 %all-reduce.26 = (f32[2,4]{0,1:T(4,128)S(1)}, f32[]{:T(128)}) all-reduce(f32[2,4]{0,1:T(4,128)S(1)} %pad_maximum_fusion.162, f32[]{:T(128)} %fusion.133), channel_id=1, replica_groups=mesh['gx'=4,'gy'=8] {'gx','gy'}, use_global_device_ids=true, to_apply=%region_54.0 | all-reduce | flops 9 | bytes 72 | tf_op jit(solution)/shard_map/psum | solution.py:181
  708.7 2.6 multiply_reduce_fusion.41
  715.1 2.6 multiply_reduce_fusion.39
  725.9 3.1 multiply_reduce_fusion.29
  736.5 2.6 multiply_reduce_fusion.19
  740.9 3.1 multiply_reduce_fusion.17
  749.0 2.6 multiply_reduce_fusion.15
  (490 shorter events, 229.7 us)
Async XLA Ops:
  46.7 4.3 collective-permute-start
  48.0 3.9 collective-permute-start.1
  51.9 6.5 collective-permute-start.2
  53.2 6.5 collective-permute-start.3
  61.0 4.3 collective-permute-start.4
  62.3 3.9 collective-permute-start.5
  66.2 7.0 collective-permute-start.6
  67.5 6.9 collective-permute-start.7
  133.6 4.3 collective-permute-start.8
  134.9 3.9 collective-permute-start.9
  138.9 6.3 collective-permute-start.10
  140.2 6.3 collective-permute-start.11
  197.9 4.3 collective-permute-start.12
  199.2 3.9 collective-permute-start.13
  203.1 6.5 collective-permute-start.14
  204.4 6.4 collective-permute-start.15
  213.1 4.7 collective-permute-start.16
  214.4 4.5 collective-permute-start.17
  218.9 7.1 collective-permute-start.18
  220.2 6.6 collective-permute-start.19
  289.2 4.3 collective-permute-start.20
  290.5 3.9 collective-permute-start.21
  294.4 6.3 collective-permute-start.22
  295.7 6.3 collective-permute-start.23
  356.1 4.3 collective-permute-start.24
  357.4 3.9 collective-permute-start.25
  361.3 6.5 collective-permute-start.26
  362.6 6.4 collective-permute-start.27
  370.7 4.6 collective-permute-start.28
  372.0 4.2 collective-permute-start.29
  376.2 6.9 collective-permute-start.30
  377.5 6.6 collective-permute-start.31
  447.1 4.4 collective-permute-start.32
  448.4 3.9 collective-permute-start.33
  452.3 6.3 collective-permute-start.34
  453.6 6.3 collective-permute-start.35
  520.9 5.8 collective-permute-start.36
  522.2 4.5 collective-permute-start.37
  526.7 6.6 collective-permute-start.38
  528.0 6.5 collective-permute-start.39
  536.2 4.6 collective-permute-start.40
  537.5 4.0 collective-permute-start.41
  541.5 7.1 collective-permute-start.42
  542.8 6.8 collective-permute-start.43
  614.3 4.4 collective-permute-start.44
  615.6 3.9 collective-permute-start.45
  619.5 6.3 collective-permute-start.46
  620.8 6.3 collective-permute-start.47
  (68 other events, 938.6 us)
where the time goes:
time: 821 us; the launch traced here: 810 us
  blocking collectives  406 us (49%)
  other arithmetic  135 us (16%)
  starting transfers between devices  129 us (16%)
  between operations  54.6 us (7%)
  matrix products  39.1 us (5%)
  waiting for transfers between devices  23 us (3%)
  local copies, waits for them, and re-layouts  22.3 us (3%)
    psum x4, blocking collectives, coarse_fix(): whole = lax.psum(padded, ('gx', 'gy'))  189 us
    psum x4, blocking collectives, body(): dots, squared = lax.psum((local_dots, jnp.sum(image * image)), ('gx', 'gy'))  175 us
    ppermute x24, starting transfers between devices, with_halo(): lax.ppermute(lax.slice_in_dim(block, block.shape[dim] - width, None, axis...  98.4 us
    reduce_sum x34, other arithmetic, least_squares(): weight = jnp.sum(ortho[position] * vector)  64.5 us
    psum x1, blocking collectives, body(): lax.psum(jnp.sum(right_side * right_side), ('gx', 'gy')) + epsilon  42.2 us
    ppermute x24, starting transfers between devices, with_halo(): lax.ppermute(lax.slice_in_dim(block, 0, width, axis=dim), axis, backward)  31 us
    dot_general x16, matrix products, accumulate(): lax.dot_general(piece, onehot, (((1,), (1,)), ((), ())), precision=lax.Pr...  27.2 us
    ppermute x24, waiting for transfers between devices, with_halo(): lax.ppermute(lax.slice_in_dim(block, block.shape[dim] - width, None, axis...  22.9 us
  transfers between devices with their start and end apart: 48, of which 23 were waited for; matrix products, arithmetic and copies ran while one was open for 1% of the time, Pallas kernels for 0%

commit v1 on v0

--- a/solution.py
+++ b/solution.py
@@ -141,7 +141,8 @@
     padded = lax.dynamic_update_slice(
         jnp.zeros((2, total_coarse), jnp.float32), partial_value, (jnp.zeros((), jnp.int32), offset)
     )
-    whole = lax.psum(padded, ("gx", "gy"))
+    terms = lax.all_gather(padded, ("gx", "gy"))
+    whole = jnp.sum(terms, axis=0)
     own_re = jnp.dot(coarse_inverse[0], whole[0], precision=highest) - jnp.dot(
         coarse_inverse[1], whole[1], precision=highest
     )

time: 821 us -> 913 us (1.11)
  blocking collectives: 406 us -> 498 us
    all_gather x0 -> x4, blocking collectives: none -> 285 us  [coarse_fix(): terms = lax.all_gather(padded, ('gx', 'gy'))]
    psum x4 -> x0, blocking collectives: 189 us -> none  [coarse_fix(): whole = lax.psum(padded, ('gx', 'gy'))]
  transfers between devices with their start and end apart: 48 -> 48, of which waited for: 23 -> 23; matrix products, arithmetic and copies ran while one was open for 1% -> 0% of each run, Pallas kernels for 0% -> 0%
where the time goes in v1:
time: 913 us; the launch traced here: 902 us
  blocking collectives  498 us (55%)
  other arithmetic  135 us (15%)
  starting transfers between devices  128 us (14%)
  between operations  54.6 us (6%)
  matrix products  39.1 us (4%)
  waiting for transfers between devices  23.6 us (3%)
  local copies, waits for them, and re-layouts  23.1 us (3%)
    all_gather x4, blocking collectives, coarse_fix(): terms = lax.all_gather(padded, ('gx', 'gy'))  285 us
    psum x4, blocking collectives, body(): dots, squared = lax.psum((local_dots, jnp.sum(image * image)), ('gx', 'gy'))  171 us
    ppermute x24, starting transfers between devices, with_halo(): lax.ppermute(lax.slice_in_dim(block, block.shape[dim] - width, None, axis...  96.9 us
    reduce_sum x34, other arithmetic, least_squares(): weight = jnp.sum(ortho[position] * vector)  64.5 us
    psum x1, blocking collectives, body(): lax.psum(jnp.sum(right_side * right_side), ('gx', 'gy')) + epsilon  42.2 us
    ppermute x24, starting transfers between devices, with_halo(): lax.ppermute(lax.slice_in_dim(block, 0, width, axis=dim), axis, backward)  31 us
    dot_general x16, matrix products, accumulate(): lax.dot_general(piece, onehot, (((1,), (1,)), ((), ())), precision=lax.Pr...  27.1 us
    ppermute x24, waiting for transfers between devices, with_halo(): lax.ppermute(lax.slice_in_dim(block, block.shape[dim] - width, None, axis...  23.5 us
  transfers between devices with their start and end apart: 48, of which 23 were waited for; matrix products, arithmetic and copies ran while one was open for 0% of the time, Pallas kernels for 0%

profile of v1, /device:TPU:0, one launch (start us, length us, event | category | flops | bytes accessed | tf_op | source)
XLA Modules:
  0.0 902.1 jit_solution(9483321204612995208)
XLA Ops:
  2.5 42.2 %psum.63 = f32[]{:T(128)} all-reduce(f32[]{:T(128)} %multiply_reduce_fusion.3), channel_id=1, replica_groups=mesh['gx'=4,'gy'=8] {'gx','gy'}, use_global_device_ids=true, to_apply=%region_1.0 | all-reduce | flops 1 | bytes 8 | tf_op jit(solution)/shard_map/psum | solution.py:169
  48.0 3.0 collective-permute-start.1
  53.2 5.0 collective-permute-start.3
  62.3 3.0 collective-permute-start.5
  67.5 5.4 collective-permute-start.7
  76.2 6.9 while.117
  83.3 71.8 %all_gather.28 = f32[32,2,512]{2,1,0:T(2,128)S(1)} all-gather(f32[1,2,512]{2,1,0:T(2,128)S(1)} %dynamic_update_slice.44), channel_id=1, replica_groups=mesh['gx'=4,'gy'=8] {'gx','gy'}, dimensions={0}, use_global_device_ids=true | all-gather | bytes 135168 | tf_op jit(solution)/shard_map/all_gather | solution.py:144
  161.1 3.0 collective-permute-start.9
  166.3 4.5 collective-permute-start.11
  175.6 41.4 %all-reduce.29 = (f32[2,1]{0,1:T(1,128)S(1)}, f32[]{:T(128)}) all-reduce(f32[2,1]{0,1:T(1,128)S(1)} %maximum_bitcast_fusion.1, f32[]{:T(128)} %multiply_reduce_fusion.2), channel_id=1, replica_groups=mesh['gx'=4,'gy'=8] {'gx','gy'}, use_global_device_ids=true, to_apply=%region_9.0 | all-reduce | flops 3 | bytes 24 | tf_op jit(solution)/shard_map/psum | solution.py:182
  222.7 3.0 collective-permute-start.13
  227.9 5.0 collective-permute-start.15
  237.8 3.4 collective-permute-start.17
  243.6 5.4 collective-permute-start.19
  251.7 2.1 divide_subtract_fusion.2
  253.8 6.9 while.118
  260.9 71.4 %all_gather.30 = f32[32,2,512]{2,1,0:T(2,128)S(1)} all-gather(f32[1,2,512]{2,1,0:T(2,128)S(1)} %dynamic_update_slice.45), channel_id=1, replica_groups=mesh['gx'=4,'gy'=8] {'gx','gy'}, dimensions={0}, use_global_device_ids=true | all-gather | bytes 135168 | tf_op jit(solution)/shard_map/all_gather | solution.py:144
  337.8 3.0 collective-permute-start.21
  343.0 4.5 collective-permute-start.23
  354.0 42.7 %all-reduce.28 = (f32[2,2]{0,1:T(2,128)S(1)}, f32[]{:T(128)}) all-reduce(f32[2,2]{0,1:T(2,128)S(1)} %pad_maximum_fusion.166, f32[]{:T(128)} %multiply_reduce_fusion.1), channel_id=1, replica_groups=mesh['gx'=4,'gy'=8] {'gx','gy'}, use_global_device_ids=true, to_apply=%region_22.0 | all-reduce | flops 5 | bytes 40 | tf_op jit(solution)/shard_map/psum | solution.py:182
  403.6 3.0 collective-permute-start.25
  408.8 5.0 collective-permute-start.27
  418.2 3.4 collective-permute-start.29
  423.8 5.2 collective-permute-start.31
  432.0 2.4 divide_subtract_fusion.1
  434.5 6.9 while.119
  441.6 71.2 %all_gather.32 = f32[32,2,512]{2,1,0:T(2,128)S(1)} all-gather(f32[1,2,512]{2,1,0:T(2,128)S(1)} %dynamic_update_slice.46), channel_id=1, replica_groups=mesh['gx'=4,'gy'=8] {'gx','gy'}, dimensions={0}, use_global_device_ids=true | all-gather | bytes 135168 | tf_op jit(solution)/shard_map/all_gather | solution.py:144
  518.3 3.0 collective-permute-start.33
  523.5 4.5 collective-permute-start.35
  537.0 43.5 %all-reduce.27 = (f32[2,3]{0,1:T(4,128)S(1)}, f32[]{:T(128)}) all-reduce(f32[2,3]{0,1:T(4,128)S(1)} %pad_maximum_fusion.161, f32[]{:T(128)} %multiply_reduce_fusion), channel_id=1, replica_groups=mesh['gx'=4,'gy'=8] {'gx','gy'}, use_global_device_ids=true, to_apply=%region_37.0 | all-reduce | flops 7 | bytes 56 | tf_op jit(solution)/shard_map/psum | solution.py:182
  583.1 2.5 multiply_subtract_fusion.5
  591.7 3.0 collective-permute-start.37
  597.5 5.1 collective-permute-start.39
  607.0 3.3 collective-permute-start.41
  612.4 5.2 collective-permute-start.43
  619.5 2.8 divide_subtract_fusion
  622.3 6.9 while.120
  629.5 70.3 %all_gather.34 = f32[32,2,512]{2,1,0:T(2,128)S(1)} all-gather(f32[1,2,512]{2,1,0:T(2,128)S(1)} %dynamic_update_slice.47), channel_id=1, replica_groups=mesh['gx'=4,'gy'=8] {'gx','gy'}, dimensions={0}, use_global_device_ids=true | all-gather | bytes 135168 | tf_op jit(solution)/shard_map/all_gather | solution.py:144
  701.4 4.3 while.116
  708.5 3.0 collective-permute-start.45
  713.7 4.5 collective-permute-start.47
  728.9 43.6 %all-reduce.26 = (f32[2,4]{0,1:T(4,128)S(1)}, f32[]{:T(128)}) all-reduce(f32[2,4]{0,1:T(4,128)S(1)} %pad_maximum_fusion.162, f32[]{:T(128)} %fusion.133), channel_id=1, replica_groups=mesh['gx'=4,'gy'=8] {'gx','gy'}, use_global_device_ids=true, to_apply=%region_54.0 | all-reduce | flops 9 | bytes 72 | tf_op jit(solution)/shard_map/psum | solution.py:182
  801.2 2.6 multiply_reduce_fusion.41
  807.6 2.6 multiply_reduce_fusion.39
  818.5 3.1 multiply_reduce_fusion.29
  829.1 2.6 multiply_reduce_fusion.19
  833.5 3.1 multiply_reduce_fusion.17
  841.5 2.6 multiply_reduce_fusion.15
  (494 shorter events, 231.3 us)
Async XLA Ops:
  46.7 4.3 collective-permute-start
  48.0 3.9 collective-permute-start.1
  51.9 6.5 collective-permute-start.2
  53.2 6.5 collective-permute-start.3
  61.0 4.3 collective-permute-start.4
  62.3 3.9 collective-permute-start.5
  66.2 7.0 collective-permute-start.6
  67.5 6.9 collective-permute-start.7
  159.8 4.3 collective-permute-start.8
  161.1 3.9 collective-permute-start.9
  165.0 6.1 collective-permute-start.10
  166.3 6.0 collective-permute-start.11
  221.4 4.3 collective-permute-start.12
  222.7 3.9 collective-permute-start.13
  226.6 6.5 collective-permute-start.14
  227.9 6.4 collective-permute-start.15
  236.5 4.7 collective-permute-start.16
  237.8 4.5 collective-permute-start.17
  242.3 6.9 collective-permute-start.18
  243.6 6.6 collective-permute-start.19
  336.5 4.3 collective-permute-start.20
  337.8 3.9 collective-permute-start.21
  341.7 6.1 collective-permute-start.22
  343.0 6.0 collective-permute-start.23
  402.3 4.3 collective-permute-start.24
  403.6 3.9 collective-permute-start.25
  407.5 6.5 collective-permute-start.26
  408.8 6.4 collective-permute-start.27
  416.9 4.7 collective-permute-start.28
  418.2 4.3 collective-permute-start.29
  422.5 6.7 collective-permute-start.30
  423.8 6.6 collective-permute-start.31
  517.0 4.4 collective-permute-start.32
  518.3 3.9 collective-permute-start.33
  522.2 6.1 collective-permute-start.34
  523.5 6.0 collective-permute-start.35
  590.4 5.8 collective-permute-start.36
  591.7 4.5 collective-permute-start.37
  596.2 6.6 collective-permute-start.38
  597.5 6.5 collective-permute-start.39
  605.7 4.8 collective-permute-start.40
  607.0 4.1 collective-permute-start.41
  611.1 6.7 collective-permute-start.42
  612.4 6.6 collective-permute-start.43
  707.2 4.4 collective-permute-start.44
  708.5 3.9 collective-permute-start.45
  712.4 6.1 collective-permute-start.46
  713.7 6.0 collective-permute-start.47
  (68 other events, 949.8 us)
